TPU v7x, 32 devices: a whole 2x2x4 slice. The times are simulated.
32 devices in a mesh: ctx: 8 (over z, x), head: 4 (over y, core).
Axes of the slice: x: 2, y: 2, z: 4, core: 2. Of those that a mesh axis runs over, the one named last changes fastest.
Arguments:
- queries: bfloat16 [4096, 4096], P('ctx', 'head'), may hold values from -6 to 6
- keys: bfloat16 [2, 4096, 4096], P(None, 'ctx', 'head'), may hold values from -6 to 6
- values: bfloat16 [2, 4096, 4096], P(None, 'ctx', 'head'), may hold values from -6 to 6
- betas: float32 [32, 2, 4096], P('head', None, 'ctx'), may hold values from 1.9 to 2
- gate: bfloat16 [4096, 4096], P('ctx', 'head'), may hold values from -6 to 6
- out_weight: bfloat16 [4096, 4096], P('head'), may hold values from -0.125 to 0.125
Outputs:
- mixed: bfloat16 [4096, 4096], P('ctx', 'head')
All inputs are finite; a program needn't handle non-finite values.
Results may differ from a plain program's by a relative error of at most 0.02.
Values may be sent and summed in bfloat16 or wider, within the bound.
A program may use at most 128 MiB of HBM per device.

v0:
```python
import math

import jax
import jax.numpy as jnp
from jax import lax
from jax.sharding import PartitionSpec as P

HEAD_DIM = 128
SPAN = 64


def prefix_2(array, axis, combine, identity):
    peers, index = (lax.axis_size(axis), lax.axis_index(axis))
    everything = jax.tree.map(
        lambda part, kind: lax.all_gather(part.astype(kind), axis),
        array,
        (jnp.bfloat16, jnp.bfloat16),
    )
    start = jax.tree.map(
        lambda part, zero: jnp.broadcast_to(jnp.asarray(zero, part.dtype), part.shape),
        array,
        identity,
    )

    def hop(k, before):
        reached = k < index
        new = combine(
            before, jax.tree.map(lambda part, own: part[k].astype(own.dtype), everything, array)
        )
        return jax.tree.map(lambda a, b: jnp.where(reached, a, b), new, before)

    return lax.fori_loop(0, peers, hop, start)


def product(left, right_part):
    return jnp.matmul(left, right_part, precision=lax.Precision.HIGHEST)


def flipped(array):
    return jnp.swapaxes(array, -1, -2)


def unit_rows(array):
    array = array.astype(jnp.float32)
    return array * lax.rsqrt(jnp.sum(array * array, axis=-1, keepdims=True) + 1e-06)


def unit_lower_solve(system, right_side):
    order = system.shape[-1]
    width = math.gcd(16, order)
    eye_block = jnp.eye(width, dtype=jnp.float32)
    pieces = []
    for index in range(order // width):
        first = index * width
        rhs = right_side[..., first : first + width, :]
        if index > 0:
            rhs = rhs - product(
                system[..., first : first + width, :first], jnp.concatenate(pieces, axis=-2)
            )
        lower = system[..., first : first + width, first : first + width] - eye_block
        inverse = eye_block - lower
        power = lower
        degree = 1
        while 2 * degree < width:
            power = product(power, power)
            inverse = product(inverse, eye_block + power)
            degree = 2 * degree
        pieces.append(product(inverse, rhs))
    return jnp.concatenate(pieces, axis=-2)


def block_factors(keys_c, values_c, betas_c, queries_c):
    sub_steps = keys_c.shape[-2]
    block_tokens = queries_c.shape[-2]
    head_size = keys_c.shape[-1]
    row_index = lax.broadcasted_iota(jnp.int32, (sub_steps, sub_steps), 0)
    col_index = lax.broadcasted_iota(jnp.int32, (sub_steps, sub_steps), 1)
    strict_lower = (col_index < row_index).astype(jnp.float32)
    system = (
        jnp.eye(sub_steps, dtype=jnp.float32)
        + betas_c[..., :, None] * product(keys_c, flipped(keys_c)) * strict_lower
    )
    right_side = betas_c[..., :, None] * jnp.concatenate([keys_c, values_c], axis=-1)
    solved = unit_lower_solve(system, right_side)
    mixing = solved[..., :head_size]
    updates = solved[..., head_size:]
    query_row = lax.broadcasted_iota(jnp.int32, (block_tokens, sub_steps), 0)
    key_col = lax.broadcasted_iota(jnp.int32, (block_tokens, sub_steps), 1)
    causal = (key_col <= 2 * query_row + 1).astype(jnp.float32)
    scores = product(queries_c, flipped(keys_c)) * causal
    local_out = product(scores, updates)
    carry_map = queries_c - product(scores, mixing)
    transit = jnp.eye(head_size, dtype=jnp.float32) - product(flipped(keys_c), mixing)
    source = product(flipped(keys_c), updates)
    return (local_out, carry_map, transit, source)


def compose(earlier, later):
    return (product(later[0], earlier[0]), product(later[0], earlier[1]) + later[1])


def per_device(queries, keys, values, betas, gate, out_weight):
    tok_count = queries.shape[0]
    feature_cols = queries.shape[1]
    head_count = feature_cols // HEAD_DIM
    blocks = tok_count // SPAN
    query_seq = unit_rows(queries.reshape(blocks, SPAN, head_count, HEAD_DIM).transpose(0, 2, 1, 3))
    key_seq = unit_rows(
        keys.reshape(2, blocks, SPAN, head_count, HEAD_DIM)
        .transpose(1, 3, 2, 0, 4)
        .reshape(blocks, head_count, 2 * SPAN, HEAD_DIM)
    )
    value_seq = (
        values.astype(jnp.float32)
        .reshape(2, blocks, SPAN, head_count, HEAD_DIM)
        .transpose(1, 3, 2, 0, 4)
        .reshape(blocks, head_count, 2 * SPAN, HEAD_DIM)
    )
    beta_seq = (
        betas.reshape(head_count, 2, blocks, SPAN)
        .transpose(2, 0, 3, 1)
        .reshape(blocks, head_count, 2 * SPAN)
    )
    local_out, carry_map, transit, source = block_factors(key_seq, value_seq, beta_seq, query_seq)
    identity = (
        jnp.broadcast_to(jnp.eye(HEAD_DIM, dtype=jnp.float32), (head_count, HEAD_DIM, HEAD_DIM)),
        jnp.zeros((head_count, HEAD_DIM, HEAD_DIM), jnp.float32),
    )

    def fold_block(carry, maps):
        return (compose(carry, maps), None)

    (shard_map_a, shard_map_b), _ = lax.scan(fold_block, identity, (transit, source))
    prefix = prefix_2((shard_map_a, shard_map_b), "ctx", compose, identity)
    start_state = prefix[1]

    def advance(state, pieces):
        local_c, carry_c, transit_c, source_c = pieces
        return (product(transit_c, state) + source_c, local_c + product(carry_c, state))

    _, outputs = lax.scan(advance, start_state, (local_out, carry_map, transit, source))
    attended = outputs.transpose(0, 2, 1, 3).reshape(tok_count, head_count, HEAD_DIM)
    scale = lax.rsqrt(jnp.mean(attended * attended, axis=-1, keepdims=True) + 1e-06)
    mixed_in = (
        attended
        * scale
        * jax.nn.silu(gate.astype(jnp.float32).reshape(tok_count, head_count, HEAD_DIM))
    ).astype(jnp.bfloat16)
    mixed_in = mixed_in.reshape(tok_count, feature_cols)
    partial_sum = jnp.dot(mixed_in, out_weight, preferred_element_type=jnp.float32)
    return lax.psum_scatter(
        partial_sum.astype(jnp.bfloat16), "head", scatter_dimension=1, tiled=True
    )


def solution(mesh):
    return jax.shard_map(
        per_device,
        mesh=mesh,
        in_specs=(
            P("ctx", "head"),
            P(None, "ctx", "head"),
            P(None, "ctx", "head"),
            P("head", None, "ctx"),
            P("ctx", "head"),
            P("head", None),
        ),
        out_specs=P("ctx", "head"),
        check_vma=False,
    )
```

profile of v0, /device:TPU:0, one launch (start us, length us, event | category | flops | bytes accessed | tf_op | source)
XLA Modules:
  0.0 383.0 jit_solution(70480197956632307)
XLA Ops:
  8.8 3.0 copy.51
  11.8 3.4 reduce_sum.27
  17.9 5.2 %copy.33 = f32[2,8,64,8,128]{4,0,2,3,1:T(2,128)} copy(f32[2,8,64,8,128]{4,3,2,1,0:T(8,128)S(1)} %bitcast.203) | data formatting | bytes 8388608 | tf_op jit(solution)/shard_map/convert_element_type | solution.py:44
  23.8 3.3 broadcast_multiply_fusion
  27.1 9.2 %multiply_add_fusion = f32[8,8,128,128]{3,2,1,0:T(8,128)S(1)} fusion(f32[8,8,128,128]{3,2,1,0:T(8,128)S(1)} %broadcast_multiply_fusion, f32[128,128]{1,0:T(8,128)S(1)} %get-tuple-element.268, f32[8,8,128]{2,1,0:T(8,128)S(1)} %copy.37, f32[128,128]{1,0:T(8,128)S(1)} %get-tuple-element.267), kind=kOutput, calls=%fused_computation.41 | convolution fusion | flops 1613758464 | bytes 8552448 | tf_op jit(solution)/shard_map/dot_general | solution.py:36
  66.8 3.3 copy.39
  72.2 2.6 constant_dynamic-update-slice_fusion.17
  92.9 3.0 copy-done.2
  100.1 2.9 constant_dynamic-update-slice_fusion.13
  103.0 4.9 %convolution_subtract_fusion.2 = f32[8,8,16,256]{3,2,1,0:T(8,128)S(1)} fusion(f32[8,8,80,256]{3,2,1,0:T(8,128)} %get-tuple-element.246, f32[8,8,128,256]{3,2,1,0:T(8,128)S(1)} %maximum_multiply_fusion, f32[8,8,128,128]{3,2,1,0:T(8,128)S(1)} %multiply_add_fusion), kind=kOutput, calls=%fused_computation.83 | convolution fusion | flops 251920384 | bytes 7864320 | tf_op jit(solution)/shard_map/dot_general | solution.py:36
  112.0 3.2 convolution_subtract_fusion.1
  119.3 6.3 %convolution_subtract_fusion = f32[8,8,16,256]{3,2,1,0:T(8,128)S(1)} fusion(f32[8,8,112,256]{3,2,1,0:T(8,128)} %get-tuple-element.238, f32[8,8,128,256]{3,2,1,0:T(8,128)S(1)} %maximum_multiply_fusion, f32[8,8,128,128]{3,2,1,0:T(8,128)S(1)} %multiply_add_fusion), kind=kOutput, calls=%fused_computation.81 | convolution fusion | flops 352583680 | bytes 9961472 | tf_op jit(solution)/shard_map/dot_general | solution.py:36
  128.6 8.8 %fusion.37 = f32[8,8,128,128]{3,2,1,0:T(8,128)} fusion(f32[8,8,128,128]{3,2,1,0:T(8,128)S(1)} %broadcast_multiply_fusion, f32[8,8,128,256]{3,2,1,0:T(8,128)S(1)} %convolution_dynamic-update-slice_fusion), kind=kOutput, calls=%fused_computation.44 | convolution fusion | flops 1610612736 | bytes 12582912 | tf_op jit(solution)/shard_map/dot_general | solution.py:36
  137.4 8.8 %fusion.49 = f32[8,8,128,128]{3,2,1,0:T(8,128)} fusion(f32[8,8,128,128]{3,2,1,0:T(8,128)S(1)} %broadcast_multiply_fusion, f32[8,8,128,256]{3,2,1,0:T(8,128)S(1)} %convolution_dynamic-update-slice_fusion, f32[128,128]{1,0:T(8,128)S(1)} %copy-done.20), kind=kOutput, calls=%fused_computation.58 | convolution fusion | flops 1611661312 | bytes 12648448 | tf_op jit(solution)/shard_map/dot_general | solution.py:36
  146.3 29.5 %while.40 = (s32[]{:T(128)}, f32[8,128,128]{2,1,0:T(8,128)S(1)}, f32[8,128,128]{2,1,0:T(8,128)S(1)}, f32[8,8,128,128]{3,2,1,0:T(8,128)}, f32[8,8,128,128]{3,2,1,0:T(8,128)}, /*index=5*/s32[]{:T(128)}, s32[]{:T(128)}) while((s32[]{:T(128)}, f32[8,128,128]{2,1,0:T(8,128)S(1)}, f32[8,128,128]{2,1,0:T(8,128)S(1)}, ...), condition=%wide.region_2.3_spmd.clone, body=%wide.region_1.0_spmd.clone.sunk | while | flops 402915328 | bytes 5768791 | solution.py:133
  179.2 10.1 %fusion.63 = f32[8,8,64,128]{3,2,1,0:T(8,128)S(1)} fusion(f32[8,8,128,128]{3,2,1,0:T(8,128)} %copy-done, f32[8,64,8,128]{3,2,1,0:T(8,128)S(1)} %bitcast.198, f32[8,8,64]{2,1,0:T(8,128)S(1)} %add_rsqrt_fusion.1), kind=kOutput, calls=%fused_computation.76 | convolution fusion | flops 805830656 | bytes 8404992 | tf_op jit(solution)/shard_map/dot_general | solution.py:36
  189.3 6.7 %fusion.35 = f32[8,8,64,128]{3,2,1,0:T(8,128)} fusion(f32[8,8,128,256]{3,2,1,0:T(8,128)} %copy-done.1, f32[8,8,64,128]{3,2,1,0:T(8,128)S(1)} %fusion.63, f32[64,128]{1,0:T(8,128)S(1)} %fusion.168), kind=kOutput, calls=%fused_computation.42 | convolution fusion | flops 805830656 | bytes 8421376 | tf_op jit(solution)/shard_map/dot_general | solution.py:36
  196.0 5.4 %fusion.62 = f32[8,8,64,128]{3,2,1,0:T(8,128)} fusion(f32[8,64,8,128]{3,2,1,0:T(8,128)S(1)} %bitcast.199, f32[8,8,128,256]{3,2,1,0:T(8,128)S(1)} %bitcast.196, f32[8,8,64,128]{3,2,1,0:T(8,128)S(1)} %fusion.63, f32[64,128]{1,0:T(8,128)S(1)} %fusion.168, f32[8,8,64]{2,1,0:T(8,128)S(1)} %add_rsqrt_fusion.1), kind=kOutput, calls=%fused_computation.75 | convolution fusion | flops 806879232 | bytes 10551296 | tf_op jit(solution)/shard_map/dot_general | solution.py:36
  201.4 27.3 %all-gather.5.cloned.1.call-done = bf16[64,128,128]{2,1,0:T(8,128)(2,1)} async-done(((bf16[8,128,128]{2,1,0:T(8,128)(2,1)}), bf16[64,128,128]{2,1,0:T(8,128)(2,1)}) %all-gather.5.cloned.1.call-update) | async-done | bytes 2097168 | tf_op jit(solution)/shard_map/all_gather | solution.py:15
  228.8 49.8 %all-gather.7.cloned.1.call-done = bf16[64,128,128]{2,1,0:T(8,128)(2,1)} async-done(((bf16[8,128,128]{2,1,0:T(8,128)(2,1)}), bf16[64,128,128]{2,1,0:T(8,128)(2,1)}) %all-gather.7.cloned.1.call-update) | async-done | bytes 2097168 | tf_op jit(solution)/shard_map/all_gather | solution.py:15
  278.6 12.7 %while.41 = (s32[]{:T(128)}, f32[8,128,128]{2,1,0:T(8,128)S(1)}, s32[]{:T(128)}, bf16[8,8,128,128]{3,2,1,0:T(8,128)(2,1)}, bf16[8,8,128,128]{3,2,1,0:T(8,128)(2,1)}, /*index=5*/s32[]{:T(128)}, s32[]{:T(128)}) while((s32[]{:T(128)}, f32[8,128,128]{2,1,0:T(8,128)S(1)}, s32[]{:T(128)}, bf16[8,8,128,128]{3,2,1,0:T(8,128)(2,1)}, ...), condition=%wide.region_4.5_spmd.clone, body=%wide.region_3.4_spmd.clone.sunk | while | flops 201981952 | bytes 3148383 | solution.py:32
  291.3 28.6 %while.39 = (s32[]{:T(128)}, f32[8,128,128]{2,1,0:T(8,128)S(1)}, f32[8,8,64,128]{3,2,1,0:T(8,128)S(1)}, f32[8,8,128,128]{3,2,1,0:T(8,128)}, f32[8,8,128,128]{3,2...) while((s32[]{:T(128)}, f32[8,128,128]{2,1,0:T(8,128)S(1)}, ...), condition=%wide.region_7.8_spmd, body=%wide.region_6.7_spmd.sunk | while | flops 302186496 | bytes 4458581 | solution.py:141
  322.5 10.6 %convolution_convert_fusion = bf16[512,4096]{1,0:T(8,128)(2,1)} fusion(bf16[1024,4096]{1,0:T(8,128)(2,1)} %param.17, bf16[512,1024]{1,0:T(8,128)(2,1)} %param.16, f32[64,8,8,128]{3,2,1,0:T(8,128)S(1)} %bitcast.209, f32[64,8,8,128]{3,2,1,0:T(8,128)S(1)} %bitcast.210), kind=kOutput, calls=%fused_computation.32 | convolution fusion | flops 4301258752 | bytes 17825792 | tf_op jit(solution)/shard_map/dot_general | solution.py:150
  333.1 43.1 %reduce-scatter.2.cloned.1.call-done = bf16[512,1024]{1,0:T(8,128)(2,1)} async-done(((bf16[512,4096]{1,0:T(8,128)(2,1)}), bf16[512,1024]{1,0:T(8,128)(2,1)}) %reduce-scatter.2.cloned.1.call-update) | async-done | bytes 1048592 | tf_op jit(solution)/shard_map/reduce_scatter | solution.py:151
  (215 shorter events, 146.7 us)
Async XLA Ops:
  6.5 222.2 %all-gather.5.cloned.1.call-start = ((), (), s32[]{:S(2)}) async-start(), calls=%async_computation.2 | async-start | bytes 2359296 | tf_op jit(solution)/shard_map/all_gather | solution.py:15
  6.6 20.5 %copy-start.19 = (f32[128,128]{1,0:T(8,128)}, f32[128,128]{1,0:T(8,128)S(1)}, u32[]{:S(2)}) copy-start(f32[128,128]{1,0:T(8,128)S(1)} %get-tuple-element.267) | copy-start | bytes 196612
  17.9 5.2 %copy-start.22 = (f32[8,2,512]{2,1,0:T(2,128)S(1)}, f32[8,2,512]{2,1,0:T(2,128)}, u32[]{:S(2)}) copy-start(f32[8,2,512]{2,1,0:T(2,128)} %param.15) | copy-start | bytes 98308
  27.1 110.3 %copy-start = (f32[8,8,128,128]{3,2,1,0:T(8,128)}, f32[8,8,128,128]{3,2,1,0:T(8,128)S(1)}, u32[]{:S(2)}) copy-start(f32[8,8,128,128]{3,2,1,0:T(8,128)S(1)} %broadcast_multiply_fusion) | copy-start | bytes 12582916
  59.1 7.0 %copy-start.9 = (bf16[2,512,1024]{2,1,0:T(8,128)(2,1)S(1)}, bf16[2,512,1024]{2,1,0:T(8,128)(2,1)}, u32[]{:S(2)}) copy-start(bf16[2,512,1024]{2,1,0:T(8,128)(2,1)} %param.14) | copy-start | bytes 6291460
  72.2 3.7 copy-start.7
  77.9 3.9 %copy-start.6 = (f32[8,8,16,16]{3,2,1,0:T(8,128)S(1)}, f32[8,8,16,16]{3,2,1,0:T(8,128)}, u32[]{:S(2)}) copy-start(f32[8,8,16,16]{3,2,1,0:T(8,128)} %fusion.178) | copy-start | bytes 196612
  80.5 1.9 copy-start.15
  86.3 2.6 copy-start.14
  92.9 3.0 copy-start.2
  95.9 2.2 copy-start.4
  95.9 2.9 copy-start.13
  103.0 5.6 %copy-start.12 = (f32[8,8,16,16]{3,2,1,0:T(8,128)S(1)}, f32[8,8,16,16]{3,2,1,0:T(8,128)}, u32[]{:S(2)}) copy-start(f32[8,8,16,16]{3,2,1,0:T(8,128)} %fusion.106) | copy-start | bytes 196612
  103.0 6.9 %copy-start.3 = (f32[8,8,96,256]{3,2,1,0:T(8,128)S(1)}, f32[8,8,96,256]{3,2,1,0:T(8,128)}, u32[]{:S(2)}) copy-start(f32[8,8,96,256]{3,2,1,0:T(8,128)} %get-tuple-element.245) | copy-start | bytes 18874372
  112.0 3.9 %copy-start.11 = (f32[8,8,16,16]{3,2,1,0:T(8,128)S(1)}, f32[8,8,16,16]{3,2,1,0:T(8,128)}, u32[]{:S(2)}) copy-start(f32[8,8,16,16]{3,2,1,0:T(8,128)} %fusion.101) | copy-start | bytes 196612
  119.3 7.0 %copy-start.10 = (f32[8,8,16,16]{3,2,1,0:T(8,128)S(1)}, f32[8,8,16,16]{3,2,1,0:T(8,128)}, u32[]{:S(2)}) copy-start(f32[8,8,16,16]{3,2,1,0:T(8,128)} %fusion.96) | copy-start | bytes 196612
  128.6 8.8 %copy-start.1 = (f32[8,8,128,256]{3,2,1,0:T(8,128)}, f32[8,8,128,256]{3,2,1,0:T(8,128)S(1)}, u32[]{:S(2)}) copy-start(f32[8,8,128,256]{3,2,1,0:T(8,128)S(1)} %convolution_dynamic-update-slice_fusion) | copy-start | bytes 25165828
  128.6 8.8 %copy-start.20 = (f32[128,128]{1,0:T(8,128)S(1)}, f32[128,128]{1,0:T(8,128)}, u32[]{:S(2)}) copy-start(f32[128,128]{1,0:T(8,128)} %copy-done.19) | copy-start | bytes 196612
  146.3 31.4 %copy-start.21 = (bf16[512,1024]{1,0:T(8,128)(2,1)S(1)}, bf16[512,1024]{1,0:T(8,128)(2,1)}, u32[]{:S(2)}) copy-start(bf16[512,1024]{1,0:T(8,128)(2,1)} %param.12) | copy-start | bytes 3145732
  176.6 101.9 %all-gather.7.cloned.1.call-start = ((), (), s32[]{:S(2)}) async-start(), calls=%async_computation.3 | async-start | bytes 2359296 | tf_op jit(solution)/shard_map/all_gather | solution.py:15
  177.4 198.8 %reduce-scatter.2.cloned.1.call-start = ((), (), s32[]{:S(2)}) async-start(), calls=%async_computation.1 | async-start | bytes 5242880 | tf_op jit(solution)/shard_map/reduce_scatter | solution.py:151
  179.1 16.8 %slice-start = ((s8[8388608]{0:T(1024)(128)(4,1)}), s8[4194304]{0:T(1024)(128)(4,1)S(1)}, s32[]{:S(2)}) async-start(s8[8388608]{0:T(1024)(128)(4,1)} %bitcast.195), calls=%async_computation.4 | async-start | bytes 8388608
  189.2 6.8 %slice-start.1 = ((s8[8388608]{0:T(1024)(128)(4,1)}), s8[4194304]{0:T(1024)(128)(4,1)S(1)}, s32[]{:S(2)}) async-start(s8[8388608]{0:T(1024)(128)(4,1)} %bitcast.195), calls=%async_computation.5 | async-start | bytes 8388608
  278.6 12.8 %copy-start.8 = (f32[8,8,64,128]{3,2,1,0:T(8,128)S(1)}, f32[8,8,64,128]{3,2,1,0:T(8,128)}, u32[]{:S(2)}) copy-start(f32[8,8,64,128]{3,2,1,0:T(8,128)} %custom-call.6) | copy-start | bytes 6291460
  (4 other events, 6.7 us)
Sparse Core Ops, SparseCore 0:
  176.7 52.0 all-gather.4
  230.9 47.6 all-gather.6
  333.2 42.9 reduce-scatter.1
where the time goes:
time: 390 us; the launch traced here: 383 us
  matrix products  212 us (54%)
  waiting for transfers between devices  120 us (31%)
  local copies, waits for them, and re-layouts  22 us (6%)
  between operations  14.1 us (4%)
  other arithmetic  13.5 us (3%)
    dot_general x109, matrix products, product(): return jnp.matmul(left, right_part, precision=lax.Precision.HIGHEST)  201 us
    all_gather x2, waiting for transfers between devices, prefix_2(): lax.all_gather(part.astype(kind), axis)  77.1 us
    reduce_scatter x1, waiting for transfers between devices, per_device(): lax.psum_scatter(partial_sum.astype(jnp.bfloat16), 'head', scatter_dimens...  43.1 us
    dot_general x1, matrix products, per_device(): jnp.dot(mixed_in, out_weight, preferred_element_type=jnp.float32)  10.6 us
    unnamed x54, local copies, waits for them, and re-layouts  9.32 us
  transfers between devices with their start and end apart: 3, of which 3 were waited for; matrix products, arithmetic and copies ran while one was open for 6% of the time, Pallas kernels for 0%

commit v1 on v0

v1 whole, which is shorter than its diff:
```python
import functools

import jax
import jax.numpy as jnp
from jax import lax
from jax.experimental import pallas as pl
from jax.experimental.pallas import tpu as pltpu
from jax.sharding import PartitionSpec as P

HEAD_DIM = 128
SPAN = 64
BASE = 16
F32 = jnp.float32
BF16 = jnp.bfloat16
VMEM_LIMIT = 60 * 1024 * 1024


def iota(shape, dim):
    return lax.broadcasted_iota(jnp.int32, shape, dim)


def split(a):
    high = a.astype(BF16)
    return high, (a - high.astype(F32)).astype(BF16)


def dot(a, b):
    return jnp.dot(a, b, preferred_element_type=F32)


def dot3(a, b):
    ah, al = split(a)
    bh, bl = split(b)
    return dot(jnp.concatenate([ah, al, ah], axis=1), jnp.concatenate([bh, bh, bl], axis=0))


def inverse(lowers, order):
    lane = iota((BASE, order), 1)
    compact = []
    for low in lowers:
        total = jnp.zeros((BASE, order), F32)
        for blk in range(order // BASE):
            total = jnp.where(lane // BASE == blk, low[blk * BASE : (blk + 1) * BASE, :], total)
        compact.append(total)
    inv = [(iota((BASE, order), 0) == lane % BASE).astype(F32) for _ in lowers]
    for j in range(BASE - 1):
        pick = (lane // BASE) * BASE + j
        for n, low in enumerate(compact):
            column = jnp.take_along_axis(low, pick, axis=1, mode="promise_in_bounds")
            inv[n] = inv[n] - column * inv[n][j : j + 1, :]
    row = iota((order, order), 0)
    col = iota((order, order), 1)
    width = BASE
    while width < order:
        corner = (row // (2 * width) == col // (2 * width)) & (row // width != col // width)
        diagonal = row // width == col // width
        second = (iota((width, order), 1) // width) % 2 == 1
        half = [dot3(jnp.where(second, t, 0.0), jnp.where(corner, low, 0.0)) for t, low in zip(inv, lowers)]
        full = [
            jnp.where(diagonal, jnp.concatenate([t] * (order // width), axis=0), 0.0) for t in inv
        ]
        fill = [dot3(y, e) for y, e in zip(half, full)]
        inv = [
            jnp.concatenate([jnp.where(second, 0.0, t), jnp.where(second, t, 0.0) - r], axis=0)
            for t, r in zip(inv, fill)
        ]
        width *= 2
    return inv


def mix_kernel(q_ref, k_ref, v_ref, b_ref, o_ref, m_ref, x_out, x_ref):
    heads = q_ref.shape[1] // HEAD_DIM
    span = q_ref.shape[0]
    order = 2 * span
    step = pl.program_id(0)

    @pl.when(step == 0)
    def _():
        start = (iota((HEAD_DIM, 2 * HEAD_DIM), 0) == iota((HEAD_DIM, 2 * HEAD_DIM), 1)).astype(F32)
        for h in range(heads):
            x_ref[h] = start

    row = iota((order, order), 0)
    col = iota((order, order), 1)
    strict = col < row
    weave = (row == 2 * (col % span) + col // span).astype(BF16)
    causal = iota((span, order), 1) <= 2 * iota((span, order), 0) + 1
    data = []
    lowers = []
    for h in range(heads):
        cols = slice(h * HEAD_DIM, (h + 1) * HEAD_DIM)
        query = q_ref[:, cols]
        pair = jnp.concatenate(
            [
                jnp.concatenate([k_ref[0, :, cols], v_ref[0, :, cols]], axis=1),
                jnp.concatenate([k_ref[1, :, cols], v_ref[1, :, cols]], axis=1),
            ],
            axis=0,
        )
        woven = dot(weave, pair)
        key = woven[:, :HEAD_DIM]
        value = woven[:, HEAD_DIM:]
        key_b = key.astype(BF16)
        norm = lax.rsqrt(jnp.sum(key * key, axis=1, keepdims=True) + 1e-06)
        beta = b_ref[:, h : h + 1]
        both = jnp.concatenate([key_b, query], axis=0)
        gram = lax.dot_general(both, key_b, (((1,), (1,)), ((), ())), preferred_element_type=F32)
        weight = beta * norm * norm
        lowers.append(jnp.where(strict, weight * gram[:order], 0.0))
        scores = jnp.where(causal, gram[order:], 0.0).astype(BF16)
        qf = query.astype(F32)
        q_norm = lax.rsqrt(jnp.sum(qf * qf, axis=1, keepdims=True) + 1e-06)
        readers = jnp.concatenate([key.T.astype(BF16), scores], axis=0)
        data.append((both, readers, beta * norm * value, weight, q_norm))
    solved = inverse(lowers, order)
    seen = []
    for h in range(heads):
        both = data[h][0]
        high, low = split(x_ref[h])
        seen.append(
            dot(jnp.concatenate([both, both], axis=1), jnp.concatenate([high, low], axis=0))
        )
    writes = []
    for h in range(heads):
        _, _, scaled, weight, _ = data[h]
        gap = -weight * seen[h][:order]
        gap = jnp.concatenate([gap[:, :HEAD_DIM], gap[:, HEAD_DIM:] + scaled], axis=1)
        writes.append(dot3(solved[h], gap))
    for h in range(heads):
        cols = slice(h * HEAD_DIM, (h + 1) * HEAD_DIM)
        readers, q_norm = data[h][1], data[h][4]
        high, low = split(writes[h])
        change = dot(
            jnp.concatenate([readers, readers], axis=1), jnp.concatenate([high, low], axis=0)
        )
        x_ref[h] = x_ref[h] + change[:HEAD_DIM]
        out = q_norm * (seen[h][order:] + change[HEAD_DIM:])
        m_ref[:, cols] = out[:, :HEAD_DIM].astype(BF16)
        o_ref[:, cols] = out[:, HEAD_DIM:]

    @pl.when(step == pl.num_programs(0) - 1)
    def _():
        for h in range(heads):
            x_out[h] = x_ref[h].astype(BF16)


def mix(queries, keys, values, beta_cols):
    tokens, width = queries.shape
    heads = width // HEAD_DIM
    return pl.pallas_call(
        mix_kernel,
        grid=(tokens // SPAN,),
        in_specs=[
            pl.BlockSpec((SPAN, width), lambda c: (c, 0)),
            pl.BlockSpec((2, SPAN, width), lambda c: (0, c, 0)),
            pl.BlockSpec((2, SPAN, width), lambda c: (0, c, 0)),
            pl.BlockSpec((2 * SPAN, heads), lambda c: (c, 0)),
        ],
        out_specs=[
            pl.BlockSpec((SPAN, width), lambda c: (c, 0)),
            pl.BlockSpec((SPAN, width), lambda c: (c, 0)),
            pl.BlockSpec((heads, HEAD_DIM, 2 * HEAD_DIM), lambda c: (0, 0, 0)),
        ],
        out_shape=[
            jax.ShapeDtypeStruct((tokens, width), F32),
            jax.ShapeDtypeStruct((tokens, width), BF16),
            jax.ShapeDtypeStruct((heads, HEAD_DIM, 2 * HEAD_DIM), BF16),
        ],
        scratch_shapes=[pltpu.VMEM((heads, HEAD_DIM, 2 * HEAD_DIM), F32)],
        compiler_params=pltpu.CompilerParams(
            dimension_semantics=("arbitrary",), vmem_limit_bytes=VMEM_LIMIT
        ),
    )(queries, keys, values, beta_cols)


def chain_kernel(peers, x_ref, s_ref):
    heads = x_ref.shape[0] // peers
    for h in range(heads):
        state = jnp.zeros((HEAD_DIM, HEAD_DIM), F32)
        for k in range(peers):
            s_ref[k * heads + h] = state.astype(BF16)
            if k < peers - 1:
                maps = x_ref[k * heads + h]
                turn = maps[:, :HEAD_DIM]
                high, low = split(state)
                state = maps[:, HEAD_DIM:].astype(F32) + dot(
                    jnp.concatenate([turn, turn], axis=1), jnp.concatenate([high, low], axis=0)
                )


def start_state(maps, axis):
    peers, index = lax.axis_size(axis), lax.axis_index(axis)
    heads = maps.shape[0]
    spread = heads % peers == 0
    if spread:
        held = lax.all_to_all(maps, axis, split_axis=0, concat_axis=0, tiled=True)
    else:
        held = lax.all_gather(maps, axis, axis=0, tiled=True)
    states = pl.pallas_call(
        functools.partial(chain_kernel, peers),
        out_shape=jax.ShapeDtypeStruct((held.shape[0], HEAD_DIM, HEAD_DIM), BF16),
        compiler_params=pltpu.CompilerParams(vmem_limit_bytes=VMEM_LIMIT),
    )(held)
    if spread:
        return lax.all_to_all(states, axis, split_axis=0, concat_axis=0, tiled=True)
    return lax.dynamic_slice_in_dim(states, index * heads, heads, 0)


def out_kernel(o_ref, m_ref, s_ref, g_ref, w_ref, y_ref, mixed_ref):
    @pl.when(pl.program_id(0) == 0)
    def _():
        for h in range(s_ref.shape[0]):
            cols = slice(h * HEAD_DIM, (h + 1) * HEAD_DIM)
            seen = o_ref[:, cols] + dot(m_ref[:, cols], s_ref[h])
            scale = lax.rsqrt(jnp.mean(seen * seen, axis=1, keepdims=True) + 1e-06)
            gate = g_ref[:, cols].astype(F32)
            mixed_ref[:, cols] = (seen * scale * (gate / (1.0 + jnp.exp(-gate)))).astype(BF16)

    y_ref[...] = dot(mixed_ref[...], w_ref[...]).astype(BF16)


def project(local, reach, states, gate, out_weight):
    tokens, width = local.shape
    total = out_weight.shape[1]
    tile = 512
    whole = pl.BlockSpec((tokens, width), lambda n: (0, 0))
    return pl.pallas_call(
        out_kernel,
        grid=(total // tile,),
        in_specs=[
            whole,
            whole,
            pl.BlockSpec(states.shape, lambda n: (0, 0, 0)),
            whole,
            pl.BlockSpec((width, tile), lambda n: (0, n)),
        ],
        out_specs=pl.BlockSpec((tokens, tile), lambda n: (0, n)),
        out_shape=jax.ShapeDtypeStruct((tokens, total), BF16),
        scratch_shapes=[pltpu.VMEM((tokens, width), BF16)],
        compiler_params=pltpu.CompilerParams(
            dimension_semantics=("arbitrary",), vmem_limit_bytes=VMEM_LIMIT
        ),
    )(local, reach, states, gate, out_weight)


def per_device(queries, keys, values, betas, gate, out_weight):
    heads, _, tokens = betas.shape
    beta_cols = betas.transpose(2, 1, 0).reshape(2 * tokens, heads)
    local, reach, maps = mix(queries, keys, values, beta_cols)
    states = start_state(maps, "ctx")
    partial_sum = project(local, reach, states, gate, out_weight)
    return lax.psum_scatter(partial_sum, "head", scatter_dimension=1, tiled=True)


def solution(mesh):
    return jax.shard_map(
        per_device,
        mesh=mesh,
        in_specs=(
            P("ctx", "head"),
            P(None, "ctx", "head"),
            P(None, "ctx", "head"),
            P("head", None, "ctx"),
            P("ctx", "head"),
            P("head", None),
        ),
        out_specs=P("ctx", "head"),
        check_vma=False,
    )
```

time: 390 us -> 140 us (0.36); the launches traced: 383 us -> 140 us
  matrix products: 212 us -> 0 us
  waiting for transfers between devices: 120 us -> 43.5 us
  Pallas kernels: 0 us -> 46.6 us
  blocking collectives: 0 us -> 34.3 us
  local copies, waits for them, and re-layouts: 22 us -> 1.75 us
  other arithmetic: 13.5 us -> 0 us
    dot_general x110 -> x0, matrix products: 212 us -> none  [the longest x109 201 us: product(): return jnp.matmul(left, right_part, precision=lax.Precision.HIGHEST)]
    all_gather x2 -> x0, waiting for transfers between devices: 77.1 us -> none  [prefix_2(): lax.all_gather(part.astype(kind), axis)]
    pallas_call x0 -> x3, Pallas kernels: none -> 46.6 us  [the longest x1 30.9 us: mix(): pl.pallas_call(mix_kernel, grid=(tokens // SPAN,), in_specs=[pl.BlockSpec...]
    all_to_all x0 -> x2, blocking collectives: none -> 34.3 us  [the longest x1 21.9 us: start_state(): held = lax.all_to_all(maps, axis, split_axis=0, concat_axis=0, tiled=True)]
    unnamed x54 -> x0, local copies, waits for them, and re-layouts: 9.32 us -> none
    mul x3 -> x0, other arithmetic: 7 us -> none  [the longest x1 3.33 us: unit_rows(): array * lax.rsqrt(jnp.sum(array * array, axis=-1, keepdims=True) + 1e-06)]
    convert_element_type x1 -> x0, local copies, waits for them, and re-layouts: 5.23 us -> none  [unit_rows(): array = array.astype(jnp.float32)]
    reduce_sum x3 -> x0, other arithmetic: 4.6 us -> none  [the longest x2 3.99 us: unit_rows(): jnp.sum(array * array, axis=-1, keepdims=True) + 1e-06]
  transfers between devices with their start and end apart: 3 -> 1, of which waited for: 3 -> 1; matrix products, arithmetic and copies ran while one was open for 6% -> 0% of each run, Pallas kernels for 0% -> 0%
where the time goes in v1:
time: 140 us
  Pallas kernels  46.6 us (33%)
  waiting for transfers between devices  43.5 us (31%)
  blocking collectives  34.3 us (24%)
  between operations  13.4 us (10%)
  local copies, waits for them, and re-layouts  1.75 us (1%)
    reduce_scatter x1, waiting for transfers between devices, per_device(): lax.psum_scatter(partial_sum, 'head', scatter_dimension=1, tiled=True)  43.5 us
    pallas_call x1, Pallas kernels, mix(): pl.pallas_call(mix_kernel, grid=(tokens // SPAN,), in_specs=[pl.BlockSpec...  30.9 us
    all_to_all x1, blocking collectives, start_state(): held = lax.all_to_all(maps, axis, split_axis=0, concat_axis=0, tiled=True)  21.9 us
    pallas_call x1, Pallas kernels, project(): pl.pallas_call(out_kernel, grid=(total // tile,), in_specs=[whole, whole,...  12.8 us
    all_to_all x1, blocking collectives, start_state(): return lax.all_to_all(states, axis, split_axis=0, concat_axis=0, tiled=True)  12.4 us
    pallas_call x1, Pallas kernels, start_state(): pl.pallas_call(functools.partial(chain_kernel, peers), out_shape=jax.Shap...  2.8 us
  transfers between devices with their start and end apart: 1, of which 1 were waited for; matrix products, arithmetic and copies ran while one was open for 0% of the time, Pallas kernels for 0%

profile of v1, /device:TPU:0, one launch (start us, length us, event | category | flops | bytes accessed | tf_op | source)
XLA Modules:
  0.0 139.5 jit_solution(8778770275227100147)
XLA Ops:
  6.5 0.0 reduce-scatter.2.cloned.1.call-start
  6.5 1.8 %copy.7 = f32[512,2,8]{2,1,0:T(2,128)} copy(f32[512,2,8]{0,1,2:T(2,128)} %bitcast.3) | data formatting | bytes 65536 | tf_op jit(solution)/shard_map/transpose | solution.py:248
  8.3 30.9 %shard_map.64 = (f32[512,1024]{1,0:T(8,128)}, bf16[512,1024]{1,0:T(8,128)(2,1)}, bf16[8,128,256]{2,1,0:T(8,128)(2,1)}) custom-call(bf16[512,1024]{1,0:T(8,128)(2,1)} %q_ref.1, bf16[2,512,1024]{2,1,0:T(8,128)(2,1)} %k_ref.1, bf16[2,512,1024]{2,1,0:T(8,128)(2,1)} %v_ref.1, f32[1024,8]{1,0:T(8,128)} %bitcast.2), custom_call_target="tpu_custom_call" | custom-call | tf_op jit(solution)/shard_map/pallas_call | solution.py:150
  39.2 21.9 %all_to_all.10.x_ref = bf16[8,128,256]{2,1,0:T(8,128)(2,1)} all-to-all(bf16[8,128,256]{2,1,0:T(8,128)(2,1)} %get-tuple-element.10), channel_id=1, replica_groups=mesh['ctx'=8,'head'=4] {'ctx'}, dimensions={0} | all-to-all | bytes 1048576 | tf_op jit(solution)/shard_map/all_to_all | solution.py:196
  61.1 2.8 %shard_map.65 = bf16[8,128,128]{2,1,0:T(8,128)(2,1)} custom-call(bf16[8,128,256]{2,1,0:T(8,128)(2,1)} %all_to_all.10.x_ref), custom_call_target="tpu_custom_call" | custom-call | tf_op jit(solution)/shard_map/pallas_call | solution.py:199
  64.0 12.4 %all_to_all.11.s_ref = bf16[8,128,128]{2,1,0:T(8,128)(2,1)} all-to-all(bf16[8,128,128]{2,1,0:T(8,128)(2,1)} %shard_map.65), channel_id=1, replica_groups=mesh['ctx'=8,'head'=4] {'ctx'}, dimensions={0} | all-to-all | bytes 524288 | tf_op jit(solution)/shard_map/all_to_all | solution.py:205
  76.4 12.8 %shard_map.66 = bf16[512,4096]{1,0:T(8,128)(2,1)} custom-call(f32[512,1024]{1,0:T(8,128)} %get-tuple-element.8.o_ref, bf16[512,1024]{1,0:T(8,128)(2,1)} %get-tuple-element.9.m_ref, bf16[8,128,128]{2,1,0:T(8,128)(2,1)} %all_to_all.11.s_ref, bf16[512,1024]{1,0:T(8,128)(2,1)} %g_ref.1, bf16[1024,4096]{1,0:T(8,128)(2,1)} %w_ref.1), custom_call_target="tpu_custom_call" | custom-call | tf_op jit(solution)/shard_map/pallas_call | solution.py:227
  89.2 0.0 reduce-scatter.2.cloned.1.call-update
  89.2 43.5 %reduce-scatter.2.cloned.1.call-done = bf16[512,1024]{1,0:T(8,128)(2,1)} async-done(((bf16[512,4096]{1,0:T(8,128)(2,1)}), bf16[512,1024]{1,0:T(8,128)(2,1)}) %reduce-scatter.2.cloned.1.call-update) | async-done | bytes 1048592 | tf_op jit(solution)/shard_map/reduce_scatter | solution.py:252
Async XLA Ops:
  6.5 126.1 %reduce-scatter.2.cloned.1.call-start = ((), (), s32[]{:S(2)}) async-start(), calls=%async_computation.3 | async-start | bytes 5242880 | tf_op jit(solution)/shard_map/reduce_scatter | solution.py:252
Sparse Core Ops, SparseCore 0:
  89.3 43.3 reduce-scatter.1

commit v2 on v1

--- a/solution.py
+++ b/solution.py
@@ -13,6 +13,8 @@
 F32 = jnp.float32
 BF16 = jnp.bfloat16
 VMEM_LIMIT = 60 * 1024 * 1024
+MESH = pl.DeviceIdType.MESH
+PIECES = 4
 
 
 def iota(shape, dim):
@@ -188,22 +190,194 @@
                 )
 
 
+def exchange_kernel(axis, peers, maps_ref, own_ref, held, states, out_send, out_recv, back_send, back_recv):
+    me = lax.axis_index(axis)
+    heads = maps_ref.shape[0] // peers
+    barrier = pltpu.get_barrier_semaphore()
+    for away in range(1, peers):
+        pl.semaphore_signal(
+            barrier, inc=1, device_id={axis: lax.rem(me + away, peers)}, device_id_type=MESH
+        )
+    pl.semaphore_wait(barrier, peers - 1)
+
+    def outward(away):
+        peer = lax.rem(me + away, peers)
+        return pltpu.make_async_remote_copy(
+            src_ref=maps_ref.at[pl.ds(peer * heads, heads)],
+            dst_ref=held.at[pl.ds(me * heads, heads)],
+            send_sem=out_send.at[away],
+            recv_sem=out_recv.at[away],
+            device_id={axis: peer},
+            device_id_type=MESH,
+        )
+
+    def homeward(away):
+        peer = lax.rem(me + away, peers)
+        return pltpu.make_async_remote_copy(
+            src_ref=states.at[pl.ds(peer * heads, heads)],
+            dst_ref=own_ref.at[pl.ds(me * heads, heads)],
+            send_sem=back_send.at[away],
+            recv_sem=back_recv.at[away],
+            device_id={axis: peer},
+            device_id_type=MESH,
+        )
+
+    for away in range(1, peers):
+        outward(away).start()
+    for h in range(heads):
+        held[me * heads + h] = maps_ref[me * heads + h]
+    for away in range(1, peers):
+        outward(away).wait()
+    chain_kernel(peers, held, states)
+    for away in range(1, peers):
+        homeward(away).start()
+    for h in range(heads):
+        own_ref[me * heads + h] = states[me * heads + h]
+    for away in range(1, peers):
+        homeward(away).wait()
+
+
 def start_state(maps, axis):
     peers, index = lax.axis_size(axis), lax.axis_index(axis)
     heads = maps.shape[0]
-    spread = heads % peers == 0
-    if spread:
-        held = lax.all_to_all(maps, axis, split_axis=0, concat_axis=0, tiled=True)
-    else:
-        held = lax.all_gather(maps, axis, axis=0, tiled=True)
+    shape = (heads, HEAD_DIM, HEAD_DIM)
+    vmem = pl.BlockSpec(memory_space=pltpu.VMEM)
+    if heads % peers == 0:
+        return pl.pallas_call(
+            functools.partial(exchange_kernel, axis, peers),
+            in_specs=[vmem],
+            out_specs=vmem,
+            out_shape=jax.ShapeDtypeStruct(shape, BF16),
+            scratch_shapes=[
+                pltpu.VMEM(maps.shape, BF16),
+                pltpu.VMEM(shape, BF16),
+                pltpu.SemaphoreType.DMA((peers,)),
+                pltpu.SemaphoreType.DMA((peers,)),
+                pltpu.SemaphoreType.DMA((peers,)),
+                pltpu.SemaphoreType.DMA((peers,)),
+            ],
+            compiler_params=pltpu.CompilerParams(
+                collective_id=0, has_side_effects=True, vmem_limit_bytes=VMEM_LIMIT
+            ),
+        )(maps)
+    held = lax.all_gather(maps, axis, axis=0, tiled=True)
     states = pl.pallas_call(
         functools.partial(chain_kernel, peers),
         out_shape=jax.ShapeDtypeStruct((held.shape[0], HEAD_DIM, HEAD_DIM), BF16),
         compiler_params=pltpu.CompilerParams(vmem_limit_bytes=VMEM_LIMIT),
     )(held)
-    if spread:
-        return lax.all_to_all(states, axis, split_axis=0, concat_axis=0, tiled=True)
     return lax.dynamic_slice_in_dim(states, index * heads, heads, 0)
+
+
+def reduce_kernel(
+    axis, o_ref, m_ref, s_ref, g_ref, w_ref, y_ref,
+    mixed, weight, total, far_out, far_in, near_out, near_in, cross_out, cross_in,
+    load_sem, far_send, far_recv, near_send, near_recv, cross_send, cross_recv,
+):
+    me = lax.axis_index(axis)
+    chip, core = me // 2, me % 2
+    sibling = 2 * chip + 1 - core
+    across = 2 * (1 - chip) + core
+    beyond = 2 * (1 - chip) + 1 - core
+    width = y_ref.shape[1]
+    rows = y_ref.shape[0] // PIECES
+
+    loads = []
+    for n, owner in enumerate((beyond, across, sibling, me)):
+        loads.append(
+            pltpu.make_async_copy(
+                w_ref.at[:, pl.ds(pl.multiple_of(owner * width, width), width)],
+                weight.at[n],
+                load_sem.at[n],
+            )
+        )
+        loads[n].start()
+
+    barrier = pltpu.get_barrier_semaphore()
+    for other in (sibling, across):
+        pl.semaphore_signal(barrier, inc=1, device_id={axis: other}, device_id_type=MESH)
+    pl.semaphore_wait(barrier, 2)
+
+    def send(source, target, send_sem, recv_sem, t, device):
+        return pltpu.make_async_remote_copy(
+            src_ref=source.at[t],
+            dst_ref=target.at[t],
+            send_sem=send_sem.at[t],
+            recv_sem=recv_sem.at[t],
+            device_id={axis: device},
+            device_id_type=MESH,
+        )
+
+    def far(t):
+        return send(far_out, far_in, far_send, far_recv, t, sibling)
+
+    def near(t):
+        return send(near_out, near_in, near_send, near_recv, t, sibling)
+
+    def cross(t):
+        return send(cross_out, cross_in, cross_send, cross_recv, t, across)
+
+    def pass_on(t):
+        far(t).wait()
+        cross_out[t] = (total[t] + far_in[t].astype(F32)).astype(BF16)
+        cross(t).start()
+
+    for t in range(PIECES):
+        span = slice(t * rows, (t + 1) * rows)
+        for h in range(s_ref.shape[0]):
+            cols = slice(h * HEAD_DIM, (h + 1) * HEAD_DIM)
+            seen = o_ref[span, cols] + dot(m_ref[span, cols], s_ref[h])
+            scale = lax.rsqrt(jnp.mean(seen * seen, axis=1, keepdims=True) + 1e-06)
+            gate = g_ref[span, cols].astype(F32)
+            mixed[t, :, cols] = (seen * scale * (gate / (1.0 + jnp.exp(-gate)))).astype(BF16)
+        if t == 0:
+            loads[0].wait()
+        far_out[t] = dot(mixed[t], weight[0]).astype(BF16)
+        far(t).start()
+        if t == 0:
+            loads[1].wait()
+        total[t] = dot(mixed[t], weight[1])
+        if t > 0:
+            pass_on(t - 1)
+    loads[2].wait()
+    for t in range(PIECES):
+        near_out[t] = dot(mixed[t], weight[2]).astype(BF16)
+        near(t).start()
+        if t == 0:
+            pass_on(PIECES - 1)
+    loads[3].wait()
+    for t in range(PIECES):
+        total[t] = dot(mixed[t], weight[3])
+    for t in range(PIECES):
+        near(t).wait()
+        cross(t).wait()
+        y_ref[t * rows : (t + 1) * rows, :] = (
+            total[t] + near_in[t].astype(F32) + cross_in[t].astype(F32)
+        ).astype(BF16)
+
+
+def project_reduce(local, reach, states, gate, out_weight, axis):
+    tokens, depth = local.shape
+    width = out_weight.shape[1] // lax.axis_size(axis)
+    vmem = pl.BlockSpec(memory_space=pltpu.VMEM)
+    piece = (PIECES, tokens // PIECES, width)
+    return pl.pallas_call(
+        functools.partial(reduce_kernel, axis),
+        in_specs=[vmem, vmem, vmem, vmem, pl.BlockSpec(memory_space=pl.ANY)],
+        out_specs=vmem,
+        out_shape=jax.ShapeDtypeStruct((tokens, width), BF16),
+        scratch_shapes=[
+            pltpu.VMEM((PIECES, tokens // PIECES, depth), BF16),
+            pltpu.VMEM((4, depth, width), BF16),
+            pltpu.VMEM(piece, F32),
+        ]
+        + [pltpu.VMEM(piece, BF16)] * 6
+        + [pltpu.SemaphoreType.DMA((4,))]
+        + [pltpu.SemaphoreType.DMA((PIECES,))] * 6,
+        compiler_params=pltpu.CompilerParams(
+            collective_id=1, has_side_effects=True, vmem_limit_bytes=VMEM_LIMIT
+        ),
+    )(local, reach, states, gate, out_weight)
 
 
 def out_kernel(o_ref, m_ref, s_ref, g_ref, w_ref, y_ref, mixed_ref):
@@ -248,6 +422,8 @@
     beta_cols = betas.transpose(2, 1, 0).reshape(2 * tokens, heads)
     local, reach, maps = mix(queries, keys, values, beta_cols)
     states = start_state(maps, "ctx")
+    if lax.axis_size("head") == 4:
+        return project_reduce(local, reach, states, gate, out_weight, "head")
     partial_sum = project(local, reach, states, gate, out_weight)
     return lax.psum_scatter(partial_sum, "head", scatter_dimension=1, tiled=True)
 

time: 140 us -> 94.5 us (0.68)
  Pallas kernels: 46.6 us -> 90.2 us
  waiting for transfers between devices: 43.5 us -> 0 us
  blocking collectives: 34.3 us -> 0 us
  between operations: 13.4 us -> 0.02 us
  local copies, waits for them, and re-layouts: 1.75 us -> 4.03 us
    pallas_call x2, Pallas kernels: 15.6 us -> 59.2 us  [the longest x1 32.1 us: project_reduce(): pl.pallas_call(functools.partial(reduce_kernel, axis), in_specs=[vmem, vm...]
    reduce_scatter x1 -> x0, waiting for transfers between devices: 43.5 us -> none  [per_device(): lax.psum_scatter(partial_sum, 'head', scatter_dimension=1, tiled=True)]
    all_to_all x2 -> x0, blocking collectives: 34.3 us -> none  [the longest x1 21.9 us: start_state(): held = lax.all_to_all(maps, axis, split_axis=0, concat_axis=0, tiled=True)]
    unnamed x0 -> x1, local copies, waits for them, and re-layouts: none -> 2.26 us
  transfers between devices with their start and end apart: 1 -> 0, of which waited for: 1 -> 0; matrix products, arithmetic and copies ran while one was open for 0% -> 0% of each run, Pallas kernels for 0% -> 0%
where the time goes in v2:
time: 94.5 us; the launch traced here: 94.2 us
  Pallas kernels  90.2 us (95%)
  local copies, waits for them, and re-layouts  4.03 us (4%)
    pallas_call x1, Pallas kernels, project_reduce(): pl.pallas_call(functools.partial(reduce_kernel, axis), in_specs=[vmem, vm...  32.1 us
    pallas_call x1, Pallas kernels, mix(): pl.pallas_call(mix_kernel, grid=(tokens // SPAN,), in_specs=[pl.BlockSpec...  30.9 us
    pallas_call x1, Pallas kernels, start_state(): pl.pallas_call(functools.partial(exchange_kernel, axis, peers), in_specs=...  27.1 us
    unnamed x1, local copies, waits for them, and re-layouts  2.26 us

profile of v2, /device:TPU:0, one launch (start us, length us, event | category | flops | bytes accessed | tf_op | source)
XLA Modules:
  0.0 94.2 jit_solution(6802846867370990142)
XLA Ops:
  0.0 1.8 %copy.7 = f32[512,2,8]{2,1,0:T(2,128)} copy(f32[512,2,8]{0,1,2:T(2,128)} %bitcast.3) | data formatting | bytes 65536 | tf_op jit(solution)/shard_map/transpose | solution.py:422
  1.8 30.9 %shard_map.64 = (f32[512,1024]{1,0:T(8,128)}, bf16[512,1024]{1,0:T(8,128)(2,1)}, bf16[8,128,256]{2,1,0:T(8,128)(2,1)}) custom-call(bf16[512,1024]{1,0:T(8,128)(2,1)} %q_ref.1, bf16[2,512,1024]{2,1,0:T(8,128)(2,1)} %k_ref.1, bf16[2,512,1024]{2,1,0:T(8,128)(2,1)} %v_ref.1, f32[1024,8]{1,0:T(8,128)} %bitcast.2), custom_call_target="tpu_custom_call" | custom-call | tf_op jit(solution)/shard_map/pallas_call | solution.py:152
  32.7 27.1 %shard_map.65.s_ref = bf16[8,128,128]{2,1,0:T(8,128)(2,1)} custom-call(bf16[8,128,256]{2,1,0:T(8,128)(2,1)} %get-tuple-element.10.maps_ref), custom_call_target="tpu_custom_call" | custom-call | tf_op jit(solution)/shard_map/pallas_call | solution.py:246
  59.9 32.1 %shard_map.66 = bf16[512,1024]{1,0:T(8,128)(2,1)} custom-call(f32[512,1024]{1,0:T(8,128)} %get-tuple-element.8.o_ref, bf16[512,1024]{1,0:T(8,128)(2,1)} %get-tuple-element.9.m_ref, bf16[8,128,128]{2,1,0:T(8,128)(2,1)} %shard_map.65.s_ref, bf16[512,1024]{1,0:T(8,128)(2,1)} %g_ref.1, bf16[1024,4096]{1,0:T(8,128)(2,1)} %w_ref.1), custom_call_target="tpu_custom_call" | custom-call | tf_op jit(solution)/shard_map/pallas_call | solution.py:364
  92.0 2.3 %copy.9 = bf16[512,1024]{1,0:T(8,128)(2,1)} copy(bf16[512,1024]{1,0:T(8,128)(2,1)} %shard_map.66) | data formatting | bytes 2097152
